TPU v7x, 256 devices: a 8x8x2 block of a 8x8x16 slice. The times are simulated.
256 devices in a mesh: groups: 2 (over z), ep: 16 (over x, core), tp: 8 (over y).
Axes of the slice: x: 8, y: 8, z: 2, core: 2. Of those that a mesh axis runs over, the one named last changes fastest.
The devices are a block of a 8x8x16 slice.
Arguments:
- tokens: bfloat16 [1024, 7168], P(('groups', 'ep')), parts along dimension 0, may hold values from -6 to 6
- w_gate: bfloat16 [16, 7168, 2048], P('ep', None, 'tp'), may hold values from -0.0625 to 0.0625
- w_up: bfloat16 [16, 7168, 2048], P('ep', None, 'tp'), may hold values from -0.0625 to 0.0625
- w_down: bfloat16 [16, 2048, 7168], P('ep', 'tp'), may hold values from -0.1875 to 0.1875
- router_logits: float32 [1024, 8], P(('groups', 'ep')), parts along dimension 0, may hold values from -6 to 6
- expert_ids: int32 [1024, 8], P(('groups', 'ep')), parts along dimension 0, may hold values from 0 to 15, all different within a row; in each aligned block of 32 rows (0 to 31, 32 to 63, ...) at most 24 rows name the same one
- draft_lengths: int32 [128], P(('groups', 'ep')), parts along dimension 0, may hold values from 7 to 8
- accept_mask: int32 [128, 8], P(('groups', 'ep')), parts along dimension 0, may hold values 0 or 1
Outputs:
- mixed: bfloat16 [1024, 7168], P(('groups', 'ep'), 'tp'), parts along dimension 0
- accepted: int32 [2], P('groups'), parts along dimension 0
There are 2 independent parts, one for each index of `groups`. A program takes and returns all parts, laid end to end along the dimension named above; an argument that names none is the same for every part. Nothing has to cross between parts.
Inputs may be any that keep to these rules, and one draw needn't show every extreme that they name: `expert_ids`: each row names 8 different experts. Among the rows of one ep index (aligned blocks of 32 rows) no expert is named by more than 24 rows, and in every draw some expert is named by exactly 24 rows of some block.
All inputs are finite; a program needn't handle non-finite values. No bound on the sum of `accept_mask` on one device may be relied on, other than what follows from the above.
Results may differ from a plain program's by a relative error of at most 0.017.
Values may be sent and summed in bfloat16 or wider, within the bound.
No kernel may reach another device: no remote copies, remote signals or barrier semaphores. Data moves between devices by JAX's collectives and lax.ppermute only.
A program may use at most 128 MiB of HBM per device.

v0:
```python
import jax
import jax.numpy as jnp
from jax import lax
from jax.sharding import PartitionSpec as P

DRAFT = 8
EXPERTS = 16
CAP = 24


def sent_to_all(array, axis):
    copies = jnp.broadcast_to(array, (lax.axis_size(axis), *array.shape))
    return lax.all_to_all(copies, axis, split_axis=0, concat_axis=0, tiled=True)


def of_everyone(array, axis):
    everything = sent_to_all(array, axis)
    return jnp.sum(everything, axis=0)


def per_device(tokens, w_gate, w_up, w_down, router_logits, expert_ids, draft_lengths, accept_mask):
    tok_rows = tokens.shape[0]
    width = tokens.shape[1]
    top = expert_ids.shape[1]
    tp_count = lax.axis_size("tp")
    slice_width = width // tp_count
    live = jnp.arange(DRAFT, dtype=jnp.int32)[None, :] < draft_lengths[:, None]
    live_rows = live.reshape(tok_rows)
    live_tokens = jnp.where(live_rows[:, None], tokens, jnp.zeros((), tokens.dtype))
    sig = jax.nn.sigmoid(router_logits)
    gates = 2.827 * sig / jnp.sum(sig, axis=1, keepdims=True)
    flat_ids = expert_ids.reshape(-1)
    onehot = (flat_ids[:, None] == jnp.arange(EXPERTS, dtype=jnp.int32)[None, :]).astype(jnp.int32)
    rank = jnp.cumsum(onehot, axis=0) - 1
    slot = jnp.sum(rank * onehot, axis=1)
    target = flat_ids * CAP + slot
    source = jnp.arange(tok_rows * top, dtype=jnp.int32) // top
    own_cols = lax.dynamic_slice_in_dim(
        live_tokens, lax.axis_index("tp") * slice_width, slice_width, 1
    )
    sendbuf = jnp.zeros((EXPERTS * CAP, slice_width), tokens.dtype).at[target].set(own_cols[source])
    received = lax.all_to_all(
        sendbuf.reshape(EXPERTS, CAP, slice_width), "ep", split_axis=0, concat_axis=1, tiled=True
    )
    piece = lax.all_gather(received, "tp", axis=2, tiled=True)
    gate_sum = jnp.einsum("emd,edf->emf", piece, w_gate, preferred_element_type=jnp.float32)
    up_sum = jnp.einsum("emd,edf->emf", piece, w_up, preferred_element_type=jnp.float32)
    hidden = (jax.nn.silu(gate_sum) * up_sum).astype(jnp.bfloat16)
    partial_value = jnp.einsum("emf,efd->emd", hidden, w_down, preferred_element_type=jnp.float32)
    expert_out = lax.psum_scatter(
        partial_value.astype(jnp.bfloat16), "tp", scatter_dimension=2, tiled=True
    )
    returned = lax.all_to_all(expert_out, "ep", split_axis=1, concat_axis=0, tiled=True)
    flat_back = returned.reshape(EXPERTS * CAP, returned.shape[2])
    picked = flat_back[target].reshape(tok_rows, top, returned.shape[2])
    mixed = jnp.sum(gates[:, :, None] * picked.astype(jnp.float32), axis=1).astype(jnp.bfloat16)
    passed = accept_mask * live.astype(jnp.int32)
    prefix = jnp.cumprod(passed, axis=1)
    local_count = jnp.sum(prefix)
    total = of_everyone(local_count, "ep")
    accepted = total.reshape(1)
    return (mixed, accepted)


def solution(mesh):
    placed = (
        P(("groups", "ep"), None),
        P("ep", None, "tp"),
        P("ep", None, "tp"),
        P("ep", "tp", None),
        P(("groups", "ep"), None),
        P(("groups", "ep"), None),
        P(("groups", "ep")),
        P(("groups", "ep"), None),
    )
    return jax.shard_map(
        per_device,
        mesh=mesh,
        in_specs=placed,
        out_specs=(P(("groups", "ep"), "tp"), P("groups")),
        check_vma=False,
    )
```

profile of v0, /device:TPU:513, one launch (start us, length us, event | category | flops | bytes accessed | tf_op | source)
XLA Modules:
  0.0 286.3 jit_solution(15594155464627464665)
XLA Ops:
  7.2 0.1 all-gather.2.cloned.1.call-start
  7.2 0.8 copy.36
  8.0 0.1 eq.29
  8.1 0.1 eq.25
  8.2 0.7 broadcast_multiply_fusion
  8.9 0.6 reduce-window.6
  9.5 0.2 slice_reduce_fusion
  9.7 0.1 copy.35
  9.8 0.1 mul.55
  9.9 0.7 iota_compare_fusion.2
  10.6 0.1 lt.48
  10.7 0.1 fusion.23
  10.8 0.9 dynamic-slice_select_fusion
  11.7 3.5 %scatter_custom_fusion = bf16[384,896]{1,0:T(8,128)(2,1)S(1)} fusion(s32[256]{0:T(256)S(1)} %bitcast.67, bf16[32,896]{1,0:T(8,128)(2,1)S(1)} %dynamic-slice_select_fusion, s32[1024]{0:T(1024)S(1)} %pad_clamp_fusion.1, bf16[]{:T(256)} %constant.43.clone.1), kind=kCustom, calls=%fused_computation.19 | custom fusion | bytes 688130 | tf_op jit(solution)/shard_map/scatter | solution.py:41
  15.2 44.7 %all_to_all.27 = bf16[16,24,896]{2,1,0:T(8,128)(2,1)} all-to-all(bf16[16,24,896]{2,1,0:T(8,128)(2,1)S(1)} %bitcast.66), channel_id=1, replica_groups=mesh['groups'=2,'ep'=16,'tp'=8] {'ep'}, dimensions={0} | all-to-all | bytes 1376256 | tf_op jit(solution)/shard_map/all_to_all | solution.py:42
  59.9 0.1 all-gather.2.cloned.1.call-update
  60.0 0.1 reduce-scatter.4.cloned.1.call-start
  60.1 66.0 %all-gather.2.cloned.1.call-done = bf16[1,384,7168]{2,1,0:T(8,128)(2,1)} async-done(((bf16[1,384,896]{2,1,0:T(8,128)(2,1)}), bf16[1,384,7168]{2,1,0:T(8,128)(2,1)}) %all-gather.2.cloned.1.call-update) | async-done | bytes 5505040 | tf_op jit(solution)/shard_map/all_gather | solution.py:45
  126.1 5.4 %fusion.3 = f32[384,256]{1,0:T(8,128)S(1)} fusion(bf16[1,384,7168]{2,1,0:T(8,128)(2,1)} %all-gather.2.cloned.1.call-done, bf16[1,7168,256]{2,1,0:T(8,128)(2,1)} %param.9), kind=kOutput, calls=%fused_computation.8 | convolution fusion | flops 1409286144 | bytes 9568256 | tf_op jit(solution)/shard_map/emd,edf->emf/dot_general | solution.py:46
  131.5 0.9 copy-done.5
  132.4 1.6 fusion.13
  134.0 0.4 copy-done
  134.4 4.0 %fusion = bf16[1,384,7168]{2,1,0:T(8,128)(2,1)} fusion(bf16[384,256]{1,0:T(8,128)(2,1)S(1)} %fusion.13, bf16[1,256,7168]{2,1,0:T(8,128)(2,1)S(1)} %copy-done), kind=kOutput, calls=%fused_computation.4 | convolution fusion | flops 1412038656 | bytes 9371648 | tf_op jit(solution)/shard_map/emf,efd->emd/dot_general | solution.py:49
  138.4 24.0 %copy.41 = bf16[1,384,7168]{1,0,2:T(2,128)(2,1)} copy(bf16[1,384,7168]{2,1,0:T(8,128)(2,1)} %fusion) | data formatting | bytes 11010048
  162.4 7.4 %copy.51 = bf16[7168,1,384]{2,0,1:T(8,128)(2,1)} copy(bf16[7168,1,384]{2,1,0:T(2,128)(2,1)} %bitcast.60) | data formatting | bytes 11010048
  169.8 0.1 reduce-scatter.4.cloned.1.call-update
  169.9 0.6 copy-done.2
  170.5 0.1 broadcast_select_fusion
  170.6 0.2 reduce_window.9
  170.8 0.6 reduce_sum.51
  171.4 1.2 broadcast_in_dim.29
  172.6 7.6 %all-to-all-start.2 = ((s32[16,1,1]{2,1,0:T(1,128)}), s32[16,1,1]{2,1,0:T(1,128)S(1)}, u32[]{:S(2)}, u32[]{:S(2)}) async-start(s32[16,1,1]{2,1,0:T(1,128)} %broadcast_in_dim.29), calls=%async_computation.2 | async-start | bytes 16384 | tf_op jit(solution)/shard_map/all_to_all | solution.py:13
  180.2 57.8 %reduce-scatter.4.cloned.1.call-done = bf16[896,384]{1,0:T(8,128)(2,1)} async-done(((bf16[7168,384]{1,0:T(8,128)(2,1)}), bf16[896,384]{1,0:T(8,128)(2,1)}) %reduce-scatter.4.cloned.1.call-update) | async-done | bytes 688144
  238.0 1.8 reshape_bitcast_fusion
  239.8 0.0 copy-start.1
  239.8 2.3 copy.39
  242.1 0.5 broadcast.160
  242.6 4.8 %reduce.3 = bf16[384,896]{1,0:T(8,128)(2,1)S(1)} reduce(bf16[384,1,896]{2,1,0:T(2,128)(2,1)S(1)} %bitcast.63, bf16[]{:T(256)} %broadcast.160), dimensions={1}, to_apply=%bitcast.54.reduce_sub_computation | reduce | bytes 1376258
  247.5 1.0 reshape.202
  248.5 0.0 all-to-all-done.2
  248.5 7.4 %all-to-all-start.1 = ((bf16[16,2,10752]{2,1,0:T(2,128)(2,1)}), bf16[16,2,10752]{2,1,0:T(2,128)(2,1)S(1)}, u32[]{:S(2)}, u32[]{:S(2)}) async-start(bf16[16,2,10752]{2,1,0:T(2,128)(2,1)} %reshape.202), calls=%async_computation.1 | async-start | bytes 1376256 | tf_op jit(solution)/shard_map/all_to_all | solution.py:53
  256.0 0.1 copy.34
  256.1 0.7 reduce_sum.52
  256.7 19.8 %all-to-all-done.1 = bf16[16,2,10752]{2,1,0:T(2,128)(2,1)S(1)} async-done(((bf16[16,2,10752]{2,1,0:T(2,128)(2,1)}), bf16[16,2,10752]{2,1,0:T(2,128)(2,1)S(1)}, u32[]{:S(2)}, u32[]{:S(2)}) %all-to-all-start.1) | async-done | bytes 688160 | tf_op jit(solution)/shard_map/all_to_all | solution.py:53
  276.6 0.6 reshape.203
  277.2 0.1 copy.52
  277.2 1.2 gather_fusion
  278.4 1.0 fusion.18
  (17 shorter events, 0.1 us)
Async XLA Ops:
  7.2 118.9 %all-gather.2.cloned.1.call-start = ((), (), s32[]{:S(2)}) async-start(), calls=%async_computation.4 | async-start | bytes 6193152 | tf_op jit(solution)/shard_map/all_gather | solution.py:45
  60.0 178.0 %reduce-scatter.4.cloned.1.call-start = ((), (), s32[]{:S(2)}) async-start(), calls=%async_computation.5 | async-start | bytes 6193152
  126.1 5.4 %copy-start.4 = (bf16[1,384,7168]{2,1,0:T(8,128)(2,1)S(1)}, bf16[1,384,7168]{2,1,0:T(8,128)(2,1)}, u32[]{:S(2)}) copy-start(bf16[1,384,7168]{2,1,0:T(8,128)(2,1)} %all-gather.2.cloned.1.call-done) | copy-start | bytes 16515076
  126.1 6.3 %copy-start.5 = (bf16[1,7168,256]{2,1,0:T(8,128)(2,1)S(1)}, bf16[1,7168,256]{2,1,0:T(8,128)(2,1)}, u32[]{:S(2)}) copy-start(bf16[1,7168,256]{2,1,0:T(8,128)(2,1)} %param.10) | copy-start | bytes 11010052
  132.4 2.0 copy-start
  169.8 0.7 copy-start.2
  169.8 0.7 copy-start.3
  172.6 75.9 %all-to-all-start.2 = ((s32[16,1,1]{2,1,0:T(1,128)}), s32[16,1,1]{2,1,0:T(1,128)S(1)}, u32[]{:S(2)}, u32[]{:S(2)}) async-start(s32[16,1,1]{2,1,0:T(1,128)} %broadcast_in_dim.29), calls=%async_computation.2 | async-start | bytes 16384 | tf_op jit(solution)/shard_map/all_to_all | solution.py:13
  239.8 16.2 %copy-start.1 = (f32[32,8]{0,1:T(8,128)S(1)}, f32[32,8]{0,1:T(8,128)}, u32[]{:S(2)}) copy-start(f32[32,8]{0,1:T(8,128)} %param.12) | copy-start | bytes 3076
  248.5 28.1 %all-to-all-start.1 = ((bf16[16,2,10752]{2,1,0:T(2,128)(2,1)}), bf16[16,2,10752]{2,1,0:T(2,128)(2,1)S(1)}, u32[]{:S(2)}, u32[]{:S(2)}) async-start(bf16[16,2,10752]{2,1,0:T(2,128)(2,1)} %reshape.202), calls=%async_computation.1 | async-start | bytes 1376256 | tf_op jit(solution)/shard_map/all_to_all | solution.py:53
Sparse Core Ops, SparseCore 0:
  60.1 65.8 all-gather.1
  170.0 67.9 reduce-scatter.3
where the time goes:
time: 288 us; the launch traced here: 286 us
  waiting for transfers between devices  144 us (50%)
  local copies, waits for them, and re-layouts  47.2 us (16%)
  blocking collectives  44.7 us (16%)
  starting transfers between devices  15.1 us (5%)
  between operations  14.2 us (5%)
  matrix products  10.9 us (4%)
  other arithmetic  10.4 us (4%)
    all_gather x1, waiting for transfers between devices, per_device(): piece = lax.all_gather(received, 'tp', axis=2, tiled=True)  66 us
    unnamed x3, waiting for transfers between devices  57.9 us
    all_to_all x1, blocking collectives, per_device(): lax.all_to_all(sendbuf.reshape(EXPERTS, CAP, slice_width), 'ep', split_ax...  44.7 us
    unnamed x20, local copies, waits for them, and re-layouts  38.2 us
    all_to_all x1, waiting for transfers between devices, per_device(): lax.all_to_all(expert_out, 'ep', split_axis=1, concat_axis=0, tiled=True)  19.8 us
    all_to_all x1, starting transfers between devices, sent_to_all(): return lax.all_to_all(copies, axis, split_axis=0, concat_axis=0, tiled=True)  7.55 us
    all_to_all x1, starting transfers between devices, per_device(): lax.all_to_all(expert_out, 'ep', split_axis=1, concat_axis=0, tiled=True)  7.44 us
  transfers between devices with their start and end apart: 4, of which 3 were waited for; matrix products, arithmetic and copies ran while one was open for 5% of the time, Pallas kernels for 0%

commit v1 on v0

--- a/solution.py
+++ b/solution.py
@@ -42,7 +42,7 @@
     received = lax.all_to_all(
         sendbuf.reshape(EXPERTS, CAP, slice_width), "ep", split_axis=0, concat_axis=1, tiled=True
     )
-    piece = lax.all_gather(received, "tp", axis=2, tiled=True)
+    piece = jnp.concatenate(lax.all_gather(received, "tp"), 2)
     gate_sum = jnp.einsum("emd,edf->emf", piece, w_gate, preferred_element_type=jnp.float32)
     up_sum = jnp.einsum("emd,edf->emf", piece, w_up, preferred_element_type=jnp.float32)
     hidden = (jax.nn.silu(gate_sum) * up_sum).astype(jnp.bfloat16)

time: 288 us -> 302 us (1.049)
  matrix products: 10.9 us -> 18.3 us
  local copies, waits for them, and re-layouts: 47.2 us -> 54 us
    dot_general x1, matrix products: 3.96 us -> 13 us  [per_device(): jnp.einsum('emf,efd->emd', hidden, w_down, preferred_element_type=jnp.flo...]
    all_gather x0 -> x1, local copies, waits for them, and re-layouts: none -> 8.27 us  [per_device(): piece = jnp.concatenate(lax.all_gather(received, 'tp'), 2)]
    unnamed x20 -> x14, local copies, waits for them, and re-layouts: 38.2 us -> 36.8 us
  transfers between devices with their start and end apart: 4 -> 4, of which waited for: 3 -> 3; matrix products, arithmetic and copies ran while one was open for 5% -> 4% of each run, Pallas kernels for 0% -> 0%
where the time goes in v1:
time: 302 us; the launch traced here: 300 us
  waiting for transfers between devices  144 us (48%)
  local copies, waits for them, and re-layouts  54 us (18%)
  blocking collectives  44.7 us (15%)
  matrix products  18.3 us (6%)
  starting transfers between devices  15.3 us (5%)
  between operations  14.2 us (5%)
  other arithmetic  10.4 us (3%)
    all_gather x1, waiting for transfers between devices, per_device(): piece = jnp.concatenate(lax.all_gather(received, 'tp'), 2)  65.8 us
    unnamed x3, waiting for transfers between devices  57.9 us
    all_to_all x1, blocking collectives, per_device(): lax.all_to_all(sendbuf.reshape(EXPERTS, CAP, slice_width), 'ep', split_ax...  44.7 us
    unnamed x14, local copies, waits for them, and re-layouts  36.8 us
    all_to_all x1, waiting for transfers between devices, per_device(): lax.all_to_all(expert_out, 'ep', split_axis=1, concat_axis=0, tiled=True)  19.8 us
    dot_general x1, matrix products, per_device(): jnp.einsum('emf,efd->emd', hidden, w_down, preferred_element_type=jnp.flo...  13 us
    all_gather x1, local copies, waits for them, and re-layouts, per_device(): piece = jnp.concatenate(lax.all_gather(received, 'tp'), 2)  8.27 us
    all_to_all x1, starting transfers between devices, sent_to_all(): return lax.all_to_all(copies, axis, split_axis=0, concat_axis=0, tiled=True)  7.55 us
  transfers between devices with their start and end apart: 4, of which 3 were waited for; matrix products, arithmetic and copies ran while one was open for 4% of the time, Pallas kernels for 0%

profile of v1, /device:TPU:513, one launch (start us, length us, event | category | flops | bytes accessed | tf_op | source)
XLA Modules:
  0.0 300.5 jit_solution(10468521131872918739)
XLA Ops:
  7.2 0.1 all-gather.2.cloned.1.call-start
  7.2 0.8 copy.45
  8.0 0.1 eq.29
  8.1 0.1 eq.25
  8.2 0.7 broadcast_multiply_fusion
  8.9 0.6 reduce-window.6
  9.5 0.2 slice_reduce_fusion
  9.7 0.1 copy.44
  9.8 0.1 mul.55
  9.9 0.7 iota_compare_fusion.2
  10.6 0.1 lt.48
  10.7 0.1 fusion.17
  10.8 0.9 dynamic-slice_select_fusion
  11.7 3.5 %scatter_custom_fusion = bf16[384,896]{1,0:T(8,128)(2,1)S(1)} fusion(s32[256]{0:T(256)S(1)} %bitcast.73, bf16[32,896]{1,0:T(8,128)(2,1)S(1)} %dynamic-slice_select_fusion, s32[1024]{0:T(1024)S(1)} %pad_clamp_fusion.1, bf16[]{:T(256)} %constant.43.clone.1), kind=kCustom, calls=%fused_computation.17 | custom fusion | bytes 688130 | tf_op jit(solution)/shard_map/scatter | solution.py:41
  15.2 44.7 %all_to_all.24 = bf16[16,24,896]{2,1,0:T(8,128)(2,1)} all-to-all(bf16[16,24,896]{2,1,0:T(8,128)(2,1)S(1)} %bitcast.72), channel_id=1, replica_groups=mesh['groups'=2,'ep'=16,'tp'=8] {'ep'}, dimensions={0} | all-to-all | bytes 1376256 | tf_op jit(solution)/shard_map/all_to_all | solution.py:42
  59.9 0.1 all-gather.2.cloned.1.call-update
  60.0 0.2 reduce-scatter.4.cloned.1.call-start
  60.3 65.8 %all-gather.2.cloned.1.call-done = bf16[8,1,384,896]{3,2,1,0:T(8,128)(2,1)} async-done(((bf16[1,1,384,896]{3,2,1,0:T(8,128)(2,1)}), bf16[8,1,384,896]{3,2,1,0:T(8,128)(2,1)}) %all-gather.2.cloned.1.call-update) | async-done | bytes 5505040 | tf_op jit(solution)/shard_map/all_gather | solution.py:45
  126.0 8.3 %copy.48 = bf16[8,1,384,896]{2,3,0,1:T(8,128)(2,1)} copy(bf16[8,1,384,896]{3,2,1,0:T(8,128)(2,1)} %all-gather.2.cloned.1.call-done) | data formatting | bytes 11010048 | tf_op jit(solution)/shard_map/all_gather | solution.py:45
  134.3 5.3 %fusion.4 = f32[384,256]{1,0:T(8,128)S(1)} fusion(bf16[384,7168]{0,1:T(8,128)(2,1)} %bitcast.64, bf16[1,7168,256]{2,1,0:T(8,128)(2,1)} %param.9), kind=kOutput, calls=%fused_computation.9 | convolution fusion | flops 1409286144 | bytes 9568256 | tf_op jit(solution)/shard_map/emd,edf->emf/dot_general | solution.py:46
  139.6 13.0 %fusion = bf16[1,384,7168]{2,1,0:T(8,128)(2,1)} fusion(bf16[1,256,7168]{2,1,0:T(8,128)(2,1)} %param.11, bf16[384,7168]{0,1:T(8,128)(2,1)} %bitcast.65, bf16[1,7168,256]{2,1,0:T(8,128)(2,1)} %param.10, f32[384,256]{1,0:T(8,128)S(1)} %fusion.4), kind=kOutput, calls=%fused_computation.4 | convolution fusion | flops 2821914624 | bytes 18743296 | tf_op jit(solution)/shard_map/emf,efd->emd/dot_general | solution.py:49
  152.6 24.0 %copy.51 = bf16[1,384,7168]{1,0,2:T(2,128)(2,1)} copy(bf16[1,384,7168]{2,1,0:T(8,128)(2,1)} %fusion) | data formatting | bytes 11010048
  176.6 7.4 %copy.61 = bf16[7168,1,384]{2,0,1:T(8,128)(2,1)} copy(bf16[7168,1,384]{2,1,0:T(2,128)(2,1)} %bitcast.66) | data formatting | bytes 11010048
  184.0 0.1 reduce-scatter.4.cloned.1.call-update
  184.1 0.6 copy-done.1
  184.7 0.0 copy-done.2
  184.7 0.1 broadcast_select_fusion
  184.8 0.2 reduce_window.9
  185.0 0.6 reduce_sum.51
  185.6 1.2 broadcast_in_dim.29
  186.8 7.6 %all-to-all-start.2 = ((s32[16,1,1]{2,1,0:T(1,128)}), s32[16,1,1]{2,1,0:T(1,128)S(1)}, u32[]{:S(2)}, u32[]{:S(2)}) async-start(s32[16,1,1]{2,1,0:T(1,128)} %broadcast_in_dim.29), calls=%async_computation.2 | async-start | bytes 16384 | tf_op jit(solution)/shard_map/all_to_all | solution.py:13
  194.4 57.8 %reduce-scatter.4.cloned.1.call-done = bf16[896,384]{1,0:T(8,128)(2,1)} async-done(((bf16[7168,384]{1,0:T(8,128)(2,1)}), bf16[896,384]{1,0:T(8,128)(2,1)}) %reduce-scatter.4.cloned.1.call-update) | async-done | bytes 688144
  252.2 1.8 reshape_bitcast_fusion
  254.0 0.0 copy-start
  254.0 2.3 copy.49
  256.3 0.5 broadcast.160
  256.8 4.8 %reduce.3 = bf16[384,896]{1,0:T(8,128)(2,1)S(1)} reduce(bf16[384,1,896]{2,1,0:T(2,128)(2,1)S(1)} %bitcast.69, bf16[]{:T(256)} %broadcast.160), dimensions={1}, to_apply=%bitcast.48.reduce_sub_computation | reduce | bytes 1376258
  261.7 1.0 reshape.210
  262.7 0.0 all-to-all-done.2
  262.7 7.4 %all-to-all-start.1 = ((bf16[16,2,10752]{2,1,0:T(2,128)(2,1)}), bf16[16,2,10752]{2,1,0:T(2,128)(2,1)S(1)}, u32[]{:S(2)}, u32[]{:S(2)}) async-start(bf16[16,2,10752]{2,1,0:T(2,128)(2,1)} %reshape.210), calls=%async_computation.1 | async-start | bytes 1376256 | tf_op jit(solution)/shard_map/all_to_all | solution.py:53
  270.1 0.0 copy-done
  270.2 0.1 copy.43
  270.3 0.7 reduce_sum.52
  270.9 19.8 %all-to-all-done.1 = bf16[16,2,10752]{2,1,0:T(2,128)(2,1)S(1)} async-done(((bf16[16,2,10752]{2,1,0:T(2,128)(2,1)}), bf16[16,2,10752]{2,1,0:T(2,128)(2,1)S(1)}, u32[]{:S(2)}, u32[]{:S(2)}) %all-to-all-start.1) | async-done | bytes 688160 | tf_op jit(solution)/shard_map/all_to_all | solution.py:53
  290.8 0.6 reshape.211
  291.3 0.1 copy.62
  291.4 1.2 gather_fusion
  292.6 1.0 fusion.12
  (11 shorter events, 0.1 us)
Async XLA Ops:
  7.2 118.9 %all-gather.2.cloned.1.call-start = ((), (), s32[]{:S(2)}) async-start(), calls=%async_computation.4 | async-start | bytes 6193152 | tf_op jit(solution)/shard_map/all_gather | solution.py:45
  60.0 192.2 %reduce-scatter.4.cloned.1.call-start = ((), (), s32[]{:S(2)}) async-start(), calls=%async_computation.5 | async-start | bytes 6193152
  184.0 0.7 copy-start.1
  184.0 0.7 copy-start.2
  186.8 75.9 %all-to-all-start.2 = ((s32[16,1,1]{2,1,0:T(1,128)}), s32[16,1,1]{2,1,0:T(1,128)S(1)}, u32[]{:S(2)}, u32[]{:S(2)}) async-start(s32[16,1,1]{2,1,0:T(1,128)} %broadcast_in_dim.29), calls=%async_computation.2 | async-start | bytes 16384 | tf_op jit(solution)/shard_map/all_to_all | solution.py:13
  254.0 16.2 %copy-start = (f32[32,8]{0,1:T(8,128)S(1)}, f32[32,8]{0,1:T(8,128)}, u32[]{:S(2)}) copy-start(f32[32,8]{0,1:T(8,128)} %param.12) | copy-start | bytes 3076
  262.7 28.1 %all-to-all-start.1 = ((bf16[16,2,10752]{2,1,0:T(2,128)(2,1)}), bf16[16,2,10752]{2,1,0:T(2,128)(2,1)S(1)}, u32[]{:S(2)}, u32[]{:S(2)}) async-start(bf16[16,2,10752]{2,1,0:T(2,128)(2,1)} %reshape.210), calls=%async_computation.1 | async-start | bytes 1376256 | tf_op jit(solution)/shard_map/all_to_all | solution.py:53
Sparse Core Ops, SparseCore 0:
  60.1 65.8 all-gather.1
  184.2 67.9 reduce-scatter.3
